TPU v7x, 128 devices: a whole 4x4x4 slice. The times are simulated.
128 devices in a mesh: tp: 8 (over y, x_hi), dp: 16 (over z, x_lo, core).
Axes of the slice: x: 4 (x_hi: 2, x_lo: 2; x = x_hi * 2 + x_lo), y: 4, z: 4, core: 2. Of those that a mesh axis runs over, the one named last changes fastest.
Arguments:
- activations: bfloat16 [2, 16384, 8192], P(None, 'dp', 'tp'), may hold values from -72 to 72
- out_grads: bfloat16 [2, 16384, 2048], P(None, 'dp'), may hold values from -2 to 2
- master: float32 [8192, 2, 2048], P(('tp', 'dp')), may hold values from -1.2 to 1.2
- first_moment: float32 [8192, 2, 2048], P(('tp', 'dp')), may hold values from -1.8 to 1.8
- second_moment: float32 [8192, 2, 2048], P(('tp', 'dp')), may hold values from 0.01 to 1
Outputs:
- new_master: float32 [8192, 2, 2048], P(('tp', 'dp'))
- new_first: float32 [8192, 2, 2048], P(('tp', 'dp'))
- new_second: float32 [8192, 2, 2048], P(('tp', 'dp'))
- weights: bfloat16 [8192, 2, 2048], P('tp')
All inputs are finite; a program needn't handle non-finite values.
Results may differ from a plain program's by a relative error of at most 0.0004.
Values may be sent and summed in bfloat16 or wider, within the bound.
A program may use at most 128 MiB of HBM per device.

v0:
```python
import functools
import math
import jax
import jax.numpy as jnp
from jax import lax
from jax.sharding import Mesh
from jax.sharding import PartitionSpec as P

DP = ("dp_0", "dp_1", "dp_2")
TP_DP = ("tp_0", "tp_1", "dp_0", "dp_1", "dp_2")
TP = ("tp_0", "tp_1")
beta_first = 0.9
beta_second = 0.95
first_fix = 1.0 - 0.9**10
second_fix = 1.0 - 0.95**10
learn_rate = 0.01
decay_rate = 0.1
epsilon = 1e-08
limit_scale = 2.0


def cut_along(array, dim, peers):
    dims = array.shape
    blocks = array.reshape(*dims[:dim], peers, dims[dim] // peers, *dims[dim + 1 :])
    return jnp.moveaxis(blocks, dim, 0)


def scatter_pairs(array, chips, core, dim):
    sizes = (lax.axis_size(chips), lax.axis_size(core))
    blocks = cut_along(array, dim, sizes[0] * sizes[1])
    inside = blocks.shape[1:]
    blocks = blocks.reshape(*sizes, *inside).swapaxes(0, 1).reshape(-1, *inside)
    blocks = lax.psum_scatter(blocks, core, scatter_dimension=0, tiled=True)
    return lax.psum_scatter(blocks, chips, scatter_dimension=0, tiled=True)[0]


def one_axis_at_a_time(array, axes):
    return functools.reduce(lax.psum, axes, array)


def reduce_rows(layer_acts, layer_grads):
    grad_own = scatter_pairs(
        jnp.einsum("ltr,ltc->rlc", layer_acts, layer_grads, preferred_element_type=jnp.float32),
        ("dp_0", "dp_1"),
        "dp_2",
        0,
    )
    partial_value = jnp.sum(grad_own * grad_own)
    return (grad_own, partial_value)


def adam_update(grad_own, master, first_moment, second_moment, clip_factor):
    clipped = clip_factor * grad_own
    new_first = beta_first * first_moment + (1.0 - beta_first) * clipped
    new_second = beta_second * second_moment + (1.0 - beta_second) * clipped * clipped
    step_dir = new_first / first_fix / (jnp.sqrt(new_second / second_fix) + epsilon)
    new_master = master - learn_rate * (step_dir + decay_rate * master)
    return (new_master, new_first, new_second)


def on_device(activations, out_grads, master, first_moment, second_moment):
    own_rows = master.shape[0]
    grad_own, layer_sum = reduce_rows(activations, out_grads)
    sum_squares = one_axis_at_a_time(layer_sum, TP_DP)
    entries = own_rows * lax.axis_size(TP) * lax.axis_size(DP) * master.shape[1] * master.shape[2]
    limit = limit_scale * math.sqrt(entries)
    clip_factor = limit / jnp.maximum(jnp.sqrt(sum_squares), limit)
    new_master, new_first, new_second = adam_update(
        grad_own, master, first_moment, second_moment, clip_factor
    )
    rounded = new_master.astype(jnp.bfloat16)
    tp_rows = lax.all_gather(rounded, DP, axis=0, tiled=True)
    return (new_master, new_first, new_second, tp_rows)


def solution(mesh):
    finer = Mesh(mesh.devices.reshape(4, 2, 4, 2, 2), ("tp_0", "tp_1", "dp_0", "dp_1", "dp_2"))
    in_specs = (
        P(None, DP, TP),
        P(None, DP, None),
        P(TP_DP, None, None),
        P(TP_DP, None, None),
        P(TP_DP, None, None),
    )
    out_specs = (
        P(TP_DP, None, None),
        P(TP_DP, None, None),
        P(TP_DP, None, None),
        P(TP, None, None),
    )
    return jax.shard_map(
        on_device, mesh=finer, in_specs=in_specs, out_specs=out_specs, check_vma=False
    )
```

profile of v0, /device:TPU:1, one launch (start us, length us, event | category | flops | bytes accessed | tf_op | source)
XLA Modules:
  0.0 349.5 jit_solution(12573614637732273600)
XLA Ops:
  7.2 0.0 reduce-scatter.3.cloned.1.call-start
  7.2 15.8 %fusion.5 = f32[2,2048,1024]{1,2,0:T(8,128)} fusion(bf16[2,1024,2048]{2,1,0:T(8,128)(2,1)} %param.6, bf16[2,1024,1024]{2,1,0:T(8,128)(2,1)} %param.5), kind=kOutput, calls=%fused_computation.9 | convolution fusion | flops 8589934592 | bytes 29360128 | tf_op jit(solution)/shard_map/ltr,ltc->rlc/dot_general | solution.py:43
  23.0 11.6 %copy.13 = f32[2,8,64,2,2048]{4,2,3,1,0:T(8,128)} copy(f32[2,8,64,2,2048]{4,2,0,1,3:T(8,128)} %bitcast.16) | data formatting | bytes 33554432 | tf_op jit(solution)/shard_map/transpose | solution.py:32
  34.7 0.0 reduce-scatter.3.cloned.1.call-update
  34.7 0.0 reduce-scatter.5.cloned.1.call-start
  34.7 31.5 %reduce-scatter.3.cloned.1.call-done = f32[8,64,2,2048]{3,1,2,0:T(8,128)} async-done(((f32[16,64,2,2048]{3,1,2,0:T(8,128)}), f32[8,64,2,2048]{3,1,2,0:T(8,128)}) %reduce-scatter.3.cloned.1.call-update) | async-done | bytes 8388624 | tf_op jit(solution)/shard_map/reduce_scatter | solution.py:33
  66.2 0.0 reduce-scatter.5.cloned.1.call-update
  66.2 0.0 all-gather.2.cloned.1.call-start
  66.3 172.5 %reduce-scatter.5.cloned.1.call-done = f32[1,64,2,2048]{3,1,2,0:T(8,128)} async-done(((f32[8,64,2,2048]{3,1,2,0:T(8,128)}), f32[1,64,2,2048]{3,1,2,0:T(8,128)}) %reduce-scatter.5.cloned.1.call-update) | async-done | bytes 1048592 | tf_op jit(solution)/shard_map/reduce_scatter | solution.py:34
  238.8 2.1 multiply_reduce_fusion
  240.9 9.1 %psum.35 = f32[]{:T(128)} all-reduce(f32[]{:T(128)} %multiply_reduce_fusion), channel_id=1, replica_groups=mesh['tp_0'=4,'tp_1'=2,'dp_0'=4,'dp_1'=2,'dp_2'=2] {'tp_0'}, use_global_device_ids=true, to_apply=%region_3.0 | all-reduce | flops 1 | bytes 8 | tf_op jit(solution)/shard_map/psum | solution.py:38
  250.0 5.9 %psum.36 = f32[]{:T(128)} all-reduce(f32[]{:T(128)} %psum.35), channel_id=1, replica_groups=mesh['tp_0'=4,'tp_1'=2,'dp_0'=4,'dp_1'=2,'dp_2'=2] {'tp_1'}, use_global_device_ids=true, to_apply=%region_4.0 | all-reduce | flops 1 | bytes 8 | tf_op jit(solution)/shard_map/psum | solution.py:38
  255.8 9.3 %psum.37 = f32[]{:T(128)} all-reduce(f32[]{:T(128)} %psum.36), channel_id=1, replica_groups=mesh['tp_0'=4,'tp_1'=2,'dp_0'=4,'dp_1'=2,'dp_2'=2] {'dp_0'}, use_global_device_ids=true, to_apply=%region_5.0 | all-reduce | flops 1 | bytes 8 | tf_op jit(solution)/shard_map/psum | solution.py:38
  265.1 4.4 %psum.38 = f32[]{:T(128)} all-reduce(f32[]{:T(128)} %psum.37), channel_id=1, replica_groups=mesh['tp_0'=4,'tp_1'=2,'dp_0'=4,'dp_1'=2,'dp_2'=2] {'dp_1'}, use_global_device_ids=true, to_apply=%region_6.0 | all-reduce | flops 1 | bytes 8 | tf_op jit(solution)/shard_map/psum | solution.py:38
  269.5 10.0 %psum.39 = f32[]{:T(128)} all-reduce(f32[]{:T(128)} %psum.38), channel_id=1, replica_groups=mesh['tp_0'=4,'tp_1'=2,'dp_0'=4,'dp_1'=2,'dp_2'=2] {'dp_2'}, use_global_device_ids=true, to_apply=%region_7.0 | all-reduce | flops 1 | bytes 8 | tf_op jit(solution)/shard_map/psum | solution.py:38
  280.3 4.5 %fusion.2 = (bf16[64,2,2048]{2,0,1:T(8,128)(2,1)S(1)}, f32[64,2,2048]{2,0,1:T(8,128)S(1)}, f32[64,2,2048]{2,0,1:T(8,128)S(1)}, f32[64,2,2048]{2,0,1:T(8,128)S(1)}) fusion(f32[64,2,2048]{2,1,0:T(2,128)} %param.7, f32[1,64,2,2048]{3,1,2,0:T(8,128)} %reduce-scatter.5.cloned.1.call-done, f32[]{:T(128)S(6)} %div.18, f32[64,2,2048]{2,1,0:T(2,128)} %param.8, ...), kind=kLoop, calls=%fused_computation.8 | loop fusion | flops 4456448 | bytes 7864324 | tf_op jit(solution)/shard_map/convert_element_type | solution.py:71
  284.8 1.3 copy.17
  286.1 0.0 all-gather.2.cloned.1.call-update
  286.1 1.8 copy.18
  287.9 1.8 copy.19
  289.7 1.8 copy.20
  291.5 43.5 %all-gather.2.cloned.1.call-done = bf16[1024,2,2048]{2,1,0:T(2,128)(2,1)} async-done(((bf16[64,2,2048]{2,1,0:T(2,128)(2,1)}), bf16[1024,2,2048]{2,1,0:T(2,128)(2,1)}) %all-gather.2.cloned.1.call-update) | async-done | bytes 8388624 | tf_op jit(solution)/shard_map/all_gather | solution.py:72
  335.0 8.0 %copy.33 = bf16[1024,2,2048]{2,1,0:T(2,128)(2,1)} copy(bf16[1024,2,2048]{2,1,0:T(2,128)(2,1)} %all-gather.2.cloned.1.call-done) | data formatting | bytes 16777216
Async XLA Ops:
  7.2 59.0 %reduce-scatter.3.cloned.1.call-start = ((), (), s32[]{:S(2)}) async-start(), calls=%async_computation.2 | async-start | bytes 25165824 | tf_op jit(solution)/shard_map/reduce_scatter | solution.py:33
  34.7 204.1 %reduce-scatter.5.cloned.1.call-start = ((), (), s32[]{:S(2)}) async-start(), calls=%async_computation.3 | async-start | bytes 9437184 | tf_op jit(solution)/shard_map/reduce_scatter | solution.py:34
  66.2 268.8 %all-gather.2.cloned.1.call-start = ((), (), s32[]{:S(2)}) async-start(), calls=%async_computation.4 | async-start | bytes 8912896 | tf_op jit(solution)/shard_map/all_gather | solution.py:72
Sparse Core Ops, SparseCore 0:
  34.8 31.3 reduce-scatter.2
  68.6 170.1 reduce-scatter.4
  286.2 48.6 all-gather.1
where the time goes:
time: 350 us; the launch traced here: 349 us
  waiting for transfers between devices  248 us (71%)
  blocking collectives  38.6 us (11%)
  local copies, waits for them, and re-layouts  26.3 us (8%)
  matrix products  15.8 us (5%)
  between operations  14.5 us (4%)
  other arithmetic  6.61 us (2%)
    reduce_scatter x1, waiting for transfers between devices, scatter_pairs(): return lax.psum_scatter(blocks, chips, scatter_dimension=0, tiled=True)[0]  173 us
    all_gather x1, waiting for transfers between devices, on_device(): tp_rows = lax.all_gather(rounded, DP, axis=0, tiled=True)  43.5 us
    psum x5, blocking collectives, one_axis_at_a_time(): return functools.reduce(lax.psum, axes, array)  38.6 us
    reduce_scatter x1, waiting for transfers between devices, scatter_pairs(): blocks = lax.psum_scatter(blocks, core, scatter_dimension=0, tiled=True)  31.5 us
    dot_general x1, matrix products, reduce_rows(): jnp.einsum('ltr,ltc->rlc', layer_acts, layer_grads, preferred_element_typ...  15.8 us
    unnamed x4, local copies, waits for them, and re-layouts  13.3 us
    transpose x1, local copies, waits for them, and re-layouts, scatter_pairs(): blocks = blocks.reshape(*sizes, *inside).swapaxes(0, 1).reshape(-1, *inside)  11.6 us
  transfers between devices with their start and end apart: 3, of which 3 were waited for; matrix products, arithmetic and copies ran while one was open for 2% of the time, Pallas kernels for 0%

commit v1 on v0

--- a/solution.py
+++ b/solution.py
@@ -17,6 +17,13 @@
 decay_rate = 0.1
 epsilon = 1e-08
 limit_scale = 2.0
+
+
+def swapped_in(shard, axis, along):
+    size = lax.axis_size(axis)
+    shards = jnp.stack([shard for _ in range(size)])
+    shards = lax.all_to_all(shards, axis, split_axis=0, concat_axis=0)
+    return jnp.concatenate(shards, axis=along)
 
 
 def cut_along(array, dim, peers):
@@ -69,7 +76,7 @@
         grad_own, master, first_moment, second_moment, clip_factor
     )
     rounded = new_master.astype(jnp.bfloat16)
-    tp_rows = lax.all_gather(rounded, DP, axis=0, tiled=True)
+    tp_rows = swapped_in(rounded, DP, 0)
     return (new_master, new_first, new_second, tp_rows)
 
 

time: 350 us -> 407 us (1.16)
  waiting for transfers between devices: 248 us -> 293 us
  local copies, waits for them, and re-layouts: 26.3 us -> 33.1 us
  starting transfers between devices: 0.12 us -> 4.92 us
    all_to_all x0 -> x1, waiting for transfers between devices: none -> 89.2 us  [swapped_in(): shards = lax.all_to_all(shards, axis, split_axis=0, concat_axis=0)]
    all_gather x1 -> x0, waiting for transfers between devices: 43.5 us -> none  [on_device(): tp_rows = lax.all_gather(rounded, DP, axis=0, tiled=True)]
    another operation x0 -> x1, local copies, waits for them, and re-layouts: none -> 7.59 us  [swapped_in(): shards = jnp.stack([shard for _ in range(size)])]
    all_to_all x0 -> x1, starting transfers between devices: none -> 4.84 us  [swapped_in(): shards = lax.all_to_all(shards, axis, split_axis=0, concat_axis=0)]
  transfers between devices with their start and end apart: 3 -> 3, of which waited for: 3 -> 3; matrix products, arithmetic and copies ran while one was open for 2% -> 1% of each run, Pallas kernels for 0% -> 0%
where the time goes in v1:
time: 407 us
  waiting for transfers between devices  293 us (72%)
  blocking collectives  38.4 us (9%)
  local copies, waits for them, and re-layouts  33.1 us (8%)
  matrix products  15.8 us (4%)
  between operations  14.8 us (4%)
  other arithmetic  6.61 us (2%)
  starting transfers between devices  4.92 us (1%)
    reduce_scatter x1, waiting for transfers between devices, scatter_pairs(): return lax.psum_scatter(blocks, chips, scatter_dimension=0, tiled=True)[0]  173 us
    all_to_all x1, waiting for transfers between devices, swapped_in(): shards = lax.all_to_all(shards, axis, split_axis=0, concat_axis=0)  89.2 us
    psum x5, blocking collectives, one_axis_at_a_time(): return functools.reduce(lax.psum, axes, array)  38.4 us
    reduce_scatter x1, waiting for transfers between devices, scatter_pairs(): blocks = lax.psum_scatter(blocks, core, scatter_dimension=0, tiled=True)  31.5 us
    dot_general x1, matrix products, reduce_rows(): jnp.einsum('ltr,ltc->rlc', layer_acts, layer_grads, preferred_element_typ...  15.8 us
    unnamed x4, local copies, waits for them, and re-layouts  13.3 us
    transpose x1, local copies, waits for them, and re-layouts, scatter_pairs(): blocks = blocks.reshape(*sizes, *inside).swapaxes(0, 1).reshape(-1, *inside)  11.6 us
  transfers between devices with their start and end apart: 3, of which 3 were waited for; matrix products, arithmetic and copies ran while one was open for 1% of the time, Pallas kernels for 0%

profile of v1, /device:TPU:1, one launch (start us, length us, event | category | flops | bytes accessed | tf_op | source)
XLA Modules:
  0.0 406.9 jit_solution(1105197506466815787)
XLA Ops:
  7.2 0.0 reduce-scatter.3.cloned.1.call-start
  7.2 15.8 %fusion.5 = f32[2,2048,1024]{1,2,0:T(8,128)} fusion(bf16[2,1024,2048]{2,1,0:T(8,128)(2,1)} %param.6, bf16[2,1024,1024]{2,1,0:T(8,128)(2,1)} %param.5), kind=kOutput, calls=%fused_computation.9 | convolution fusion | flops 8589934592 | bytes 29360128 | tf_op jit(solution)/shard_map/ltr,ltc->rlc/dot_general | solution.py:50
  23.0 11.6 %copy.13 = f32[2,8,64,2,2048]{4,2,3,1,0:T(8,128)} copy(f32[2,8,64,2,2048]{4,2,0,1,3:T(8,128)} %bitcast.17) | data formatting | bytes 33554432 | tf_op jit(solution)/shard_map/transpose | solution.py:39
  34.7 0.0 reduce-scatter.3.cloned.1.call-update
  34.7 0.0 reduce-scatter.5.cloned.1.call-start
  34.7 31.5 %reduce-scatter.3.cloned.1.call-done = f32[8,64,2,2048]{3,1,2,0:T(8,128)} async-done(((f32[16,64,2,2048]{3,1,2,0:T(8,128)}), f32[8,64,2,2048]{3,1,2,0:T(8,128)}) %reduce-scatter.3.cloned.1.call-update) | async-done | bytes 8388624 | tf_op jit(solution)/shard_map/reduce_scatter | solution.py:40
  66.2 0.0 reduce-scatter.5.cloned.1.call-update
  66.2 172.6 %reduce-scatter.5.cloned.1.call-done = f32[1,64,2,2048]{3,1,2,0:T(8,128)} async-done(((f32[8,64,2,2048]{3,1,2,0:T(8,128)}), f32[1,64,2,2048]{3,1,2,0:T(8,128)}) %reduce-scatter.5.cloned.1.call-update) | async-done | bytes 1048592 | tf_op jit(solution)/shard_map/reduce_scatter | solution.py:41
  238.8 2.1 multiply_reduce_fusion
  240.9 9.1 %psum.35 = f32[]{:T(128)} all-reduce(f32[]{:T(128)} %multiply_reduce_fusion), channel_id=1, replica_groups=mesh['tp_0'=4,'tp_1'=2,'dp_0'=4,'dp_1'=2,'dp_2'=2] {'tp_0'}, use_global_device_ids=true, to_apply=%region_3.0 | all-reduce | flops 1 | bytes 8 | tf_op jit(solution)/shard_map/psum | solution.py:45
  250.0 5.9 %psum.36 = f32[]{:T(128)} all-reduce(f32[]{:T(128)} %psum.35), channel_id=1, replica_groups=mesh['tp_0'=4,'tp_1'=2,'dp_0'=4,'dp_1'=2,'dp_2'=2] {'tp_1'}, use_global_device_ids=true, to_apply=%region_4.0 | all-reduce | flops 1 | bytes 8 | tf_op jit(solution)/shard_map/psum | solution.py:45
  255.8 9.3 %psum.37 = f32[]{:T(128)} all-reduce(f32[]{:T(128)} %psum.36), channel_id=1, replica_groups=mesh['tp_0'=4,'tp_1'=2,'dp_0'=4,'dp_1'=2,'dp_2'=2] {'dp_0'}, use_global_device_ids=true, to_apply=%region_5.0 | all-reduce | flops 1 | bytes 8 | tf_op jit(solution)/shard_map/psum | solution.py:45
  265.1 4.4 %psum.38 = f32[]{:T(128)} all-reduce(f32[]{:T(128)} %psum.37), channel_id=1, replica_groups=mesh['tp_0'=4,'tp_1'=2,'dp_0'=4,'dp_1'=2,'dp_2'=2] {'dp_1'}, use_global_device_ids=true, to_apply=%region_6.0 | all-reduce | flops 1 | bytes 8 | tf_op jit(solution)/shard_map/psum | solution.py:45
  269.5 9.8 %psum.39 = f32[]{:T(128)} all-reduce(f32[]{:T(128)} %psum.38), channel_id=1, replica_groups=mesh['tp_0'=4,'tp_1'=2,'dp_0'=4,'dp_1'=2,'dp_2'=2] {'dp_2'}, use_global_device_ids=true, to_apply=%region_7.0 | all-reduce | flops 1 | bytes 8 | tf_op jit(solution)/shard_map/psum | solution.py:45
  280.1 4.5 %fusion.2 = (bf16[64,2,2048]{2,0,1:T(8,128)(2,1)S(1)}, f32[64,2,2048]{2,0,1:T(8,128)S(1)}, f32[64,2,2048]{2,0,1:T(8,128)S(1)}, f32[64,2,2048]{2,0,1:T(8,128)S(1)}) fusion(f32[64,2,2048]{2,1,0:T(2,128)} %param.7, f32[1,64,2,2048]{3,1,2,0:T(8,128)} %reduce-scatter.5.cloned.1.call-done, f32[]{:T(128)S(6)} %div.18, f32[64,2,2048]{2,1,0:T(2,128)} %param.8, ...), kind=kLoop, calls=%fused_computation.8 | loop fusion | flops 4456448 | bytes 7864324 | tf_op jit(solution)/shard_map/convert_element_type | solution.py:78
  284.6 0.5 copy.17
  285.1 7.6 %stack.2 = bf16[16,64,2,2048]{3,2,1,0:T(2,128)(2,1)} broadcast(bf16[64,2,2048]{2,1,0:T(2,128)(2,1)S(1)} %copy.17), dimensions={1,2,3} | broadcast | bytes 8912896 | tf_op jit(solution)/shard_map/stack | solution.py:24
  292.7 4.8 %all-to-all-start = ((bf16[16,64,2,2048]{3,2,1,0:T(2,128)(2,1)}), bf16[16,64,2,2048]{3,2,1,0:T(2,128)(2,1)}, u32[]{:S(2)}, u32[]{:S(2)}) async-start(bf16[16,64,2,2048]{3,2,1,0:T(2,128)(2,1)} %stack.2), calls=%async_computation.2 | async-start | bytes 16777216 | tf_op jit(solution)/shard_map/all_to_all | solution.py:25
  297.6 1.8 copy.18
  299.3 1.8 copy.19
  301.1 1.8 copy.20
  302.9 89.2 %all-to-all-done = bf16[16,64,2,2048]{3,2,1,0:T(2,128)(2,1)} async-done(((bf16[16,64,2,2048]{3,2,1,0:T(2,128)(2,1)}), bf16[16,64,2,2048]{3,2,1,0:T(2,128)(2,1)}, u32[]{:S(2)}, u32[]{:S(2)}) %all-to-all-start) | async-done | bytes 8388640 | tf_op jit(solution)/shard_map/all_to_all | solution.py:25
  392.1 8.0 %copy.33 = bf16[1024,2,2048]{2,1,0:T(2,128)(2,1)} copy(bf16[1024,2,2048]{2,1,0:T(2,128)(2,1)} %bitcast.5) | data formatting | bytes 16777216
Async XLA Ops:
  7.2 59.0 %reduce-scatter.3.cloned.1.call-start = ((), (), s32[]{:S(2)}) async-start(), calls=%async_computation.3 | async-start | bytes 25165824 | tf_op jit(solution)/shard_map/reduce_scatter | solution.py:40
  34.7 204.1 %reduce-scatter.5.cloned.1.call-start = ((), (), s32[]{:S(2)}) async-start(), calls=%async_computation.4 | async-start | bytes 9437184 | tf_op jit(solution)/shard_map/reduce_scatter | solution.py:41
  292.7 99.4 %all-to-all-start = ((bf16[16,64,2,2048]{3,2,1,0:T(2,128)(2,1)}), bf16[16,64,2,2048]{3,2,1,0:T(2,128)(2,1)}, u32[]{:S(2)}, u32[]{:S(2)}) async-start(bf16[16,64,2,2048]{3,2,1,0:T(2,128)(2,1)} %stack.2), calls=%async_computation.2 | async-start | bytes 16777216 | tf_op jit(solution)/shard_map/all_to_all | solution.py:25
Sparse Core Ops, SparseCore 0:
  34.8 31.3 reduce-scatter.2
  68.6 170.1 reduce-scatter.4
